TPU v7x, 32 devices: a whole 2x2x4 slice. The times are simulated.
32 devices in a mesh: dp: 16 (over z, y, x), mp: 2 (over core).
Axes of the slice: x: 2, y: 2, z: 4, core: 2. Of those that a mesh axis runs over, the one named last changes fastest.
Arguments:
- hidden: bfloat16 [240, 128, 2048], P('dp', None, 'mp'), may hold values from -6 to 6
- attn_out: bfloat16 [240, 128, 2048], P('dp', None, 'mp'), may hold values from -6 to 6
- out_proj: bfloat16 [2048, 2048], P(None, 'mp'), may hold values from -0.125 to 0.125
- norm_gain: float32 [2048], P('mp'), may hold values from 0.1 to 1.9
- reward_proj: float32 [2048, 8], P('mp'), may hold values from -0.125 to 0.125
- block_seq: int32 [240], replicated, may hold values from -1 to 95, as said below
- block_dest: int32 [240], replicated, may hold values from -1 to 159, as said below
- lengths: int32 [96], replicated, may hold values from 1 to 512, as said below
Outputs:
- token_rewards: float32 [160, 8, 128], P('dp')
- advantages: float32 [96], P('dp')
Inputs may be any that keep to these rules, and one draw needn't show every extreme that they name: `block_seq`: used slots of each index of dp come first in its 15 slots, the rest hold -1; each index of dp holds 1 to 15 used slots and some index holds exactly 15. Read over used slots in slot order, response numbers never fall, every response appears, and each has 1 to 4 blocks. `block_dest`: exactly the used slots (those of block_seq that are not -1) hold a destination; every owned slot of every owner is named exactly once, so each owner receives exactly 10 blocks; at most 1 block go from one index of dp to one owner, and that many in some pair. `lengths`: A response of n blocks has more than 128 * (n - 1) and at most 128 * n tokens.
All inputs are finite; a program needn't handle non-finite values.
Results may differ from a plain program's by a relative error of at most 0.0029.
Values may be sent and summed in bfloat16 or wider, within the bound.
A program may use at most 64 MiB of HBM per device.

v0:
```python
import functools

import jax
import jax.numpy as jnp
from jax import lax
from jax.experimental import pallas as pl
from jax.experimental.pallas import tpu as pltpu
from jax.sharding import PartitionSpec as P

OWN_CAP = 10

norm_epsilon = 1e-05
stat_epsilon = 1e-06
MESH = pl.DeviceIdType.MESH
LANES = 128


def split_size(slots):
    for size in (5, 4, 3, 2):
        if slots % size == 0:
            return size
    return 1


def kernel(
    n_dp, n_mp, slots, block_len, seq_count, per_group,
    hidden_hbm, attn_hbm, w_hbm, gain_hbm, reward_hbm, seq_hbm, dest_hbm, len_hbm,
    recv_buf,
    attn, w, hidden, acc, resid, heads_w, part, live, rewards, seq_acc, send_buf,
    send_idx, gain_ref, reward_ref, seq_s, dest_s, len_s, seq_v, small_sem,
    w_sem, own_sem, hid_sem, attn_send, attn_recv, part_send, part_recv, dp_send, dp_recv,
):
    dp = lax.axis_index("dp")
    mp = lax.axis_index("mp")
    groups = slots // per_group
    rows = per_group * block_len
    k_local = attn_hbm.shape[1]
    n_local = w_hbm.shape[1]
    model_width = w_hbm.shape[0]
    chunk = min(256, n_local)
    n_chunks = n_local // chunk

    barrier = pltpu.get_barrier_semaphore()
    for off in range(1, n_mp):
        pl.semaphore_signal(barrier, inc=1, device_id=(dp, lax.rem(mp + off, n_mp)), device_id_type=MESH)
    for off in range(1, n_dp):
        pl.semaphore_signal(barrier, inc=1, device_id=(lax.rem(dp + off, n_dp), mp), device_id_type=MESH)

    def w_copy(m):
        start = pl.multiple_of(m * k_local, k_local)
        return pltpu.make_async_copy(w_hbm.at[pl.ds(start, k_local)], w.at[m], w_sem.at[m])

    def group_rows(g):
        return pl.ds(pl.multiple_of(g * rows, rows), rows)

    def own_copy(g):
        return pltpu.make_async_copy(attn_hbm.at[group_rows(g)], attn.at[mp, group_rows(g)], own_sem.at[g])

    def hid_copy(g):
        return pltpu.make_async_copy(hidden_hbm.at[group_rows(g)], hidden.at[group_rows(g)], hid_sem.at[g])

    def attn_copy(off, g):
        return pltpu.make_async_remote_copy(
            src_ref=attn_hbm.at[group_rows(g)],
            dst_ref=attn.at[mp, group_rows(g)],
            send_sem=attn_send.at[off - 1, g],
            recv_sem=attn_recv.at[off - 1, g],
            device_id=(dp, lax.rem(mp + off, n_mp)),
            device_id_type=MESH,
        )

    def part_copy(off, g):
        return pltpu.make_async_remote_copy(
            src_ref=part.at[mp, g],
            dst_ref=part.at[mp, g],
            send_sem=part_send.at[off - 1, g],
            recv_sem=part_recv.at[off - 1, g],
            device_id=(dp, lax.rem(mp + off, n_mp)),
            device_id_type=MESH,
        )

    def dp_copy(off):
        peer = lax.rem(dp + off, n_dp)
        return pltpu.make_async_remote_copy(
            src_ref=send_buf.at[peer],
            dst_ref=recv_buf.at[dp],
            send_sem=dp_send.at[off - 1],
            recv_sem=dp_recv.at[off - 1],
            device_id=(peer, mp),
            device_id_type=MESH,
        )

    small = [
        pltpu.make_async_copy(src, dst, small_sem.at[i])
        for i, (src, dst) in enumerate(
            (
                (gain_hbm, gain_ref),
                (reward_hbm, reward_ref),
                (seq_hbm, seq_s),
                (dest_hbm, dest_s),
                (len_hbm, len_s),
                (seq_hbm, seq_v),
            )
        )
    ]
    for copy in small:
        copy.start()
    w_copy(mp).start()
    for g in range(groups):
        own_copy(g).start()
    for off in range(1, n_mp):
        w_copy(lax.rem(mp + off, n_mp)).start()
    for g in range(groups):
        hid_copy(g).start()

    for copy in small:
        copy.wait()
    head_count = reward_ref.shape[0]
    weighted = reward_ref[...] * gain_ref[...].reshape(1, n_local)
    high = weighted.astype(jnp.bfloat16)
    rest = weighted - high.astype(jnp.float32)
    middle = rest.astype(jnp.bfloat16)
    low = (rest - middle.astype(jnp.float32)).astype(jnp.bfloat16)
    heads_w[...] = jnp.concatenate([high, middle, low, jnp.zeros_like(low)], axis=0)

    base = dp * slots

    def send_body(r, carry):
        low_dest = r * OWN_CAP
        found = jnp.int32(0)
        for j in range(slots):
            d = dest_s[base + j]
            found = jnp.where((d >= low_dest) & (d < low_dest + OWN_CAP), jnp.int32(j), found)
        send_idx[r] = found
        return carry

    lax.fori_loop(0, n_dp, send_body, 0)
    all_slots = seq_s.shape[0]
    slot_lane = lax.broadcasted_iota(jnp.int32, (1, all_slots), 1)
    seq_row = seq_v[...].reshape(1, all_slots)
    token = lax.broadcasted_iota(jnp.int32, (1, block_len), 1).astype(jnp.float32)
    for j in range(slots):
        seq = seq_s[base + j]
        earlier = jnp.where((seq_row == seq) & (slot_lane < base + j), 1.0, 0.0)
        rank = jnp.sum(earlier, axis=1, keepdims=True)
        length = len_s[jnp.maximum(seq, 0)].astype(jnp.float32)
        valid = length - rank * float(block_len)
        live[j : j + 1, :] = jnp.where(token < valid, 1.0, 0.0)
    seq_acc[...] = jnp.zeros_like(seq_acc)

    pl.semaphore_wait(barrier, n_mp - 1 + n_dp - 1)
    for g in range(groups):
        for off in range(1, n_mp):
            attn_copy(off, g).start()

    w_copy(mp).wait()

    def first_half(g, carry):
        own_copy(g).wait()
        for c in range(n_chunks):
            cols = slice(c * chunk, (c + 1) * chunk)
            acc[group_rows(g), cols] = jnp.dot(
                attn[mp, group_rows(g), :], w[mp, :, cols], preferred_element_type=jnp.float32
            )
        return carry

    lax.fori_loop(0, groups, first_half, 0)
    for off in range(1, n_mp):
        w_copy(lax.rem(mp + off, n_mp)).wait()

    seq_lane = lax.broadcasted_iota(jnp.int32, (head_count, seq_acc.shape[1]), 1)

    def finish(g):
        for off in range(1, n_mp):
            part_copy(off, g).wait()
        total = part[0, g]
        for m in range(1, n_mp):
            total = total + part[m, g]
        scale = lax.rsqrt(total[head_count:] / model_width + norm_epsilon)
        values = total[:head_count] * scale
        for b in range(per_group):
            j = g * per_group + b
            block = values[:, b * block_len : (b + 1) * block_len] * live[pl.ds(j, 1), :]
            rewards[j] = block
            sums = jnp.sum(block, axis=1, keepdims=True)
            seq_acc[...] += jnp.where(seq_lane == seq_s[base + j], sums, 0.0)

    def second_half(g, carry):
        hid_copy(g).wait()
        for off in range(1, n_mp):
            attn_copy(off, g).wait()
        squares = jnp.zeros((rows, LANES), jnp.float32)
        for c in range(n_chunks):
            cols = slice(c * chunk, (c + 1) * chunk)
            total = acc[group_rows(g), cols]
            for off in range(1, n_mp):
                m = lax.rem(mp + off, n_mp)
                total = total + jnp.dot(
                    attn[m, group_rows(g), :], w[m, :, cols], preferred_element_type=jnp.float32
                )
            stored = (hidden[group_rows(g), cols].astype(jnp.float32) + total).astype(jnp.bfloat16)
            resid[:, cols] = stored
            v = stored.astype(jnp.float32)
            for i in range(chunk // LANES):
                piece = v[:, i * LANES : (i + 1) * LANES]
                squares = squares + piece * piece
        heads = lax.dot_general(
            heads_w[...], resid[...], (((1,), (1,)), ((), ())), preferred_element_type=jnp.float32
        )
        h = head_count
        part[mp, g, 0:h, :] = heads[0:h] + heads[h : 2 * h] + heads[2 * h : 3 * h]
        sum_row = jnp.sum(jnp.transpose(squares), axis=0, keepdims=True)
        part[mp, g, h : 2 * h, :] = jnp.broadcast_to(sum_row, (h, rows))
        for off in range(1, n_mp):
            part_copy(off, g).start()

        @pl.when(g > 0)
        def _():
            finish(g - 1)

        return carry

    lax.fori_loop(0, groups, second_half, 0)
    finish(groups - 1)

    seq_part = seq_acc[...]

    def fill(r, carry):
        send_buf[r, :, 0:block_len] = rewards[send_idx[r]]
        send_buf[r, :, block_len:] = seq_part
        return carry

    lax.fori_loop(0, n_dp, fill, 0, unroll=n_dp <= 16)
    kept = pltpu.make_async_copy(send_buf.at[dp], recv_buf.at[dp], small_sem.at[0])
    kept.start()
    for off in range(1, n_dp):
        dp_copy(off).start()
    for off in range(1, n_dp):
        dp_copy(off).wait()
    kept.wait()


def finish_kernel(n_dp, slots, seq_count, block_len, recv_buf, dest_v, len_v, rewards_out, adv_out, adv_buf):
    dp = lax.axis_index("dp")
    all_slots = dest_v.shape[0]
    slot_lane = lax.broadcasted_iota(jnp.int32, (1, all_slots), 1)
    dest_row = dest_v[...].reshape(1, all_slots)
    for q in range(OWN_CAP):
        place = jnp.max(jnp.where(dest_row == dp * OWN_CAP + q, slot_lane, 0))
        rewards_out[q] = recv_buf[lax.div(place, slots), :, 0:block_len]
    totals = recv_buf[0, :, block_len:]
    for s in range(1, n_dp):
        totals = totals + recv_buf[s, :, block_len:]
    scores = totals[:, :seq_count] / len_v[...].reshape(1, seq_count).astype(jnp.float32)
    worst = jnp.min(scores, axis=0, keepdims=True)
    centred = scores - jnp.mean(scores, axis=0, keepdims=True)
    spread = jnp.mean(centred * centred, axis=0, keepdims=True)
    penalty_scale = jnp.mean(spread, axis=1, keepdims=True) + stat_epsilon
    conservative = worst - spread / penalty_scale
    shifted = conservative - jnp.mean(conservative, axis=1, keepdims=True)
    variance = jnp.mean(shifted * shifted, axis=1, keepdims=True)
    adv_buf[...] = jnp.zeros_like(adv_buf)
    adv_buf[0:1, :seq_count] = shifted * lax.rsqrt(variance + stat_epsilon)
    width = adv_buf.shape[1]
    seq_local = adv_out.shape[1]
    turned = pltpu.roll(adv_buf[...], width - dp * seq_local, 1)
    adv_out[...] = turned[0:1, :seq_local]

def local(n_dp, n_mp, hidden, attn_out, out_proj, norm_gain, reward_proj, block_seq, block_dest, lengths):
    slots, block_len, k_local = attn_out.shape
    n_local = out_proj.shape[1]
    seq_count = lengths.shape[0]
    seq_pad = -(-seq_count // LANES) * LANES
    heads = reward_proj.shape[1]
    per_group = split_size(slots)
    groups = slots // per_group
    rows = per_group * block_len
    total_rows = slots * block_len
    f32, bf16 = jnp.float32, jnp.bfloat16
    dma = pltpu.SemaphoreType.DMA
    any_spec = pl.BlockSpec(memory_space=pl.ANY)
    vmem_spec = pl.BlockSpec(memory_space=pltpu.VMEM)
    width = block_len + seq_pad
    received = pl.pallas_call(
        functools.partial(kernel, n_dp, n_mp, slots, block_len, seq_count, per_group),
        out_shape=jax.ShapeDtypeStruct((n_dp, heads, width), f32),
        in_specs=[any_spec] * 8,
        out_specs=any_spec,
        scratch_shapes=[
            pltpu.VMEM((n_mp, total_rows, k_local), bf16),
            pltpu.VMEM((n_mp, k_local, n_local), bf16),
            pltpu.VMEM((total_rows, n_local), bf16),
            pltpu.VMEM((total_rows, n_local), f32),
            pltpu.VMEM((rows, n_local), bf16),
            pltpu.VMEM((4 * heads, n_local), bf16),
            pltpu.VMEM((n_mp, groups, 2 * heads, rows), f32),
            pltpu.VMEM((slots + (-slots) % 8, block_len), f32),
            pltpu.VMEM((slots, heads, block_len), f32),
            pltpu.VMEM((heads, seq_pad), f32),
            pltpu.VMEM((n_dp, heads, width), f32),
            pltpu.SMEM((n_dp,), jnp.int32),
            pltpu.VMEM(norm_gain.shape, f32),
            pltpu.VMEM((heads, n_local), f32),
            pltpu.SMEM(block_seq.shape, jnp.int32),
            pltpu.SMEM(block_dest.shape, jnp.int32),
            pltpu.SMEM(lengths.shape, jnp.int32),
            pltpu.VMEM(block_seq.shape, jnp.int32),
            dma((6,)),
            dma((n_mp,)),
            dma((groups,)),
            dma((groups,)),
            dma((n_mp - 1, groups)),
            dma((n_mp - 1, groups)),
            dma((n_mp - 1, groups)),
            dma((n_mp - 1, groups)),
            dma((n_dp - 1,)),
            dma((n_dp - 1,)),
        ],
        compiler_params=pltpu.CompilerParams(
            collective_id=0, has_side_effects=True, vmem_limit_bytes=60 * 1024 * 1024
        ),
    )(
        hidden.reshape(total_rows, n_local),
        attn_out.reshape(total_rows, k_local),
        out_proj,
        norm_gain,
        reward_proj.T,
        block_seq,
        block_dest,
        lengths,
    )
    token_rewards, advantages = pl.pallas_call(
        functools.partial(finish_kernel, n_dp, slots, seq_count, block_len),
        out_shape=(
            jax.ShapeDtypeStruct((OWN_CAP, heads, block_len), f32),
            jax.ShapeDtypeStruct((1, seq_count // n_dp), f32),
        ),
        in_specs=[vmem_spec] * 3,
        out_specs=(vmem_spec, vmem_spec),
        scratch_shapes=[pltpu.VMEM((8, seq_pad), f32)],
    )(received, block_dest, lengths)
    return token_rewards, advantages.reshape(seq_count // n_dp)


def solution(mesh):
    return jax.shard_map(
        functools.partial(local, mesh.shape["dp"], mesh.shape["mp"]),
        mesh=mesh,
        in_specs=(
            P("dp", None, "mp"),
            P("dp", None, "mp"),
            P(None, "mp"),
            P("mp"),
            P("mp", None),
            P(),
            P(),
            P(),
        ),
        out_specs=(P("dp", None, None), P("dp")),
        check_vma=False,
    )
```

profile of v0, /device:TPU:0, one launch (start us, length us, event | category | flops | bytes accessed | tf_op | source)
XLA Modules:
  0.0 26.7 jit_solution(14141650369470893897)
XLA Ops:
  0.6 24.2 %shard_map.95.recv_buf = f32[16,8,256]{2,1,0:T(8,128)} custom-call(bf16[1920,1024]{1,0:T(8,128)(2,1)} %bitcast.4, bf16[1920,1024]{1,0:T(8,128)(2,1)} %bitcast.5, bf16[2048,1024]{1,0:T(8,128)(2,1)} %w_hbm.1, f32[1024]{0:T(1024)} %gain_hbm.1, f32[8,1024]{1,0:T(8,128)} %bitcast.6, s32[240]{0:T(256)} %seq_hbm.1, s32[240]{0:T(256)} %dest_v.1, s32[96]{0:T(128)} %len_v.1), custom_call_target="tpu_custom_call" | custom-call | tf_op jit(solution)/shard_map/pallas_call | solution.py:284
  24.8 1.9 %shard_map.96 = (f32[10,8,128]{2,1,0:T(8,128)}, f32[1,6]{1,0:T(1,128)}) custom-call(f32[16,8,256]{2,1,0:T(8,128)} %shard_map.95.recv_buf, s32[240]{0:T(256)} %dest_v.1, s32[96]{0:T(128)} %len_v.1), custom_call_target="tpu_custom_call" | custom-call | tf_op jit(solution)/shard_map/pallas_call | solution.py:332
where the time goes:
time: 26.9 us; the launch traced here: 26.7 us
  Pallas kernels  26.1 us (97%)
  between operations  0.64 us (2%)
    pallas_call x1, Pallas kernels, local(): pl.pallas_call(functools.partial(kernel, n_dp, n_mp, slots, block_len, se...  24.2 us
    pallas_call x1, Pallas kernels, local(): pl.pallas_call(functools.partial(finish_kernel, n_dp, slots, seq_count, b...  1.89 us

commit v1 on v0

v1 whole, which is shorter than its diff:
```python
import functools

import jax
import jax.numpy as jnp
from jax import lax
from jax.experimental import pallas as pl
from jax.experimental.pallas import tpu as pltpu
from jax.sharding import PartitionSpec as P

OWN_CAP = 10

norm_epsilon = 1e-05
stat_epsilon = 1e-06
MESH = pl.DeviceIdType.MESH
LANES = 128


def split_slots(slots):
    third = max(1, slots // 3)
    first = ((0, third), (third, slots)) if slots > third else ((0, slots),)
    cuts = [*range(0, slots - third + 1, third), slots]
    second = tuple(zip(cuts[:-1], cuts[1:]))
    return first, second, second


def partner(index, k, n):
    if n & (n - 1):
        return lax.rem(index + k, n)
    out = index
    bit = 1
    while bit < n:
        if k & bit:
            out = out + bit - 2 * bit * lax.rem(lax.div(index, bit), 2)
        bit *= 2
    return out


def kernel(
    n_dp, n_mp, slots, block_len, seq_count, groups,
    hidden_hbm, attn_hbm, w_hbm, gain_hbm, reward_hbm, seq_hbm, dest_hbm, len_hbm,
    rewards_out, adv_out,
    attn, w, hidden, acc, resid, heads_w, part, live, rewards, seq_acc, send_buf,
    recv_sum, recv_rew, adv_buf,
    send_idx, gain_ref, reward_ref, seq_s, dest_s, len_s, seq_v, dest_v, len_v, small_sem,
    w_sem, own_sem, hid_sem, attn_send, attn_recv, part_send, part_recv,
    sum_send, sum_recv, rew_send, rew_recv,
):
    dp = lax.axis_index("dp")
    mp = lax.axis_index("mp")
    first_ranges, second_ranges, head_ranges = groups
    k_local = attn_hbm.shape[1]
    n_local = w_hbm.shape[1]
    model_width = w_hbm.shape[0]
    chunk = min(256, n_local)
    n_chunks = n_local // chunk
    head_count = reward_ref.shape[0]
    h = head_count
    base = dp * slots

    barrier = pltpu.get_barrier_semaphore()
    for off in range(1, n_mp):
        pl.semaphore_signal(barrier, inc=1, device_id=(dp, lax.rem(mp + off, n_mp)), device_id_type=MESH)
    for k in range(n_dp - 1, 0, -1):
        pl.semaphore_signal(barrier, inc=1, device_id=(partner(dp, k, n_dp), mp), device_id_type=MESH)

    def block_rows(blocks):
        return slice(blocks[0] * block_len, blocks[1] * block_len)

    k_half = k_local // 2

    def w_copy(off, half):
        start = pl.multiple_of(lax.rem(mp + off, n_mp) * k_local + half * k_half, k_half)
        return pltpu.make_async_copy(
            w_hbm.at[pl.ds(start, k_half)], w.at[off, half * k_half : (half + 1) * k_half], w_sem.at[off, half]
        )

    def lead_copy(half):
        rows = block_rows(first_ranges[0])
        cols = slice(half * k_half, (half + 1) * k_half)
        return pltpu.make_async_copy(attn_hbm.at[rows, cols], attn.at[0, rows, cols], own_sem.at[half])

    def own_copy(i):
        rows = block_rows(first_ranges[i])
        return pltpu.make_async_copy(attn_hbm.at[rows], attn.at[0, rows], own_sem.at[i + 1])

    def other_w(action):
        for off in range(1, n_mp):
            for half in range(2):
                getattr(w_copy(off, half), action)()

    def hid_copy(i):
        rows = block_rows(second_ranges[i])
        return pltpu.make_async_copy(hidden_hbm.at[rows], hidden.at[rows], hid_sem.at[i])

    def attn_copy(off, i):
        rows = block_rows(second_ranges[i])
        return pltpu.make_async_remote_copy(
            src_ref=attn_hbm.at[rows],
            dst_ref=attn.at[n_mp - off, rows],
            send_sem=attn_send.at[off - 1, i],
            recv_sem=attn_recv.at[off - 1, i],
            device_id=(dp, lax.rem(mp + off, n_mp)),
            device_id_type=MESH,
        )

    def part_copy(off, i):
        rows = block_rows(head_ranges[i])
        return pltpu.make_async_remote_copy(
            src_ref=part.at[0, :, rows],
            dst_ref=part.at[n_mp - off, :, rows],
            send_sem=part_send.at[off - 1, i],
            recv_sem=part_recv.at[off - 1, i],
            device_id=(dp, lax.rem(mp + off, n_mp)),
            device_id_type=MESH,
        )

    def sum_copy(k):
        return pltpu.make_async_remote_copy(
            src_ref=seq_acc,
            dst_ref=recv_sum.at[dp],
            send_sem=sum_send,
            recv_sem=sum_recv,
            device_id=(partner(dp, k, n_dp), mp),
            device_id_type=MESH,
        )

    def rew_copy(k):
        peer = partner(dp, k, n_dp)
        return pltpu.make_async_remote_copy(
            src_ref=send_buf.at[peer],
            dst_ref=recv_rew.at[dp],
            send_sem=rew_send,
            recv_sem=rew_recv,
            device_id=(peer, mp),
            device_id_type=MESH,
        )

    def wait_all(ref, sem):
        others = ref.at[0 : n_dp - 1]
        pltpu.make_async_copy(others, others, sem).wait()

    w_copy(0, 0).start()
    lead_copy(0).start()
    small = [
        pltpu.make_async_copy(src, dst, small_sem.at[i])
        for i, (src, dst) in enumerate(
            (
                (gain_hbm, gain_ref),
                (reward_hbm, reward_ref),
                (seq_hbm, seq_s),
                (dest_hbm, dest_s),
                (len_hbm, len_s),
                (seq_hbm, seq_v),
                (dest_hbm, dest_v),
                (len_hbm, len_v),
            )
        )
    ]
    for copy in small:
        copy.start()
    with jax.named_scope("smallw"):
        small[0].wait()
        small[1].wait()
    weighted = reward_ref[...] * gain_ref[...].reshape(1, n_local)
    high = weighted.astype(jnp.bfloat16)
    rest = weighted - high.astype(jnp.float32)
    middle = rest.astype(jnp.bfloat16)
    low = (rest - middle.astype(jnp.float32)).astype(jnp.bfloat16)
    heads_w[...] = jnp.concatenate([high, middle, low, jnp.zeros_like(low)], axis=0)
    seq_acc[...] = jnp.zeros_like(seq_acc)

    def first_half(i):
        rows = block_rows(first_ranges[i])
        for c in range(n_chunks):
            cols = slice(c * chunk, (c + 1) * chunk)
            acc[rows, cols] = jnp.dot(attn[0, rows, :], w[0, :, cols], preferred_element_type=jnp.float32)

    def lead(half):
        rows = block_rows(first_ranges[0])
        depth = slice(half * k_half, (half + 1) * k_half)
        for c in range(n_chunks):
            cols = slice(c * chunk, (c + 1) * chunk)
            product = jnp.dot(attn[0, rows, depth], w[0, depth, cols], preferred_element_type=jnp.float32)
            acc[rows, cols] = acc[rows, cols] + product if half else product

    def send_attn(i):
        if i < len(second_ranges):
            for off in range(1, n_mp):
                attn_copy(off, i).start()

    w_copy(0, 1).start()
    lead_copy(1).start()
    with jax.named_scope("lead0"):
        w_copy(0, 0).wait()
        lead_copy(0).wait()
    for i in range(1, len(first_ranges)):
        own_copy(i).start()
    lead(0)
    with jax.named_scope("barr"):
        pl.semaphore_wait(barrier, n_mp - 1 + n_dp - 1)
    send_attn(0)
    with jax.named_scope("lead1"):
        w_copy(0, 1).wait()
        lead_copy(1).wait()
    lead(1)
    send_attn(1)
    other_w("start")
    for i in range(1, len(first_ranges)):
        with jax.named_scope("ownw"):
            own_copy(i).wait()
        if i == 1:
            for j in range(len(second_ranges)):
                hid_copy(j).start()
        first_half(i)
    for i in range(2, len(second_ranges)):
        send_attn(i)

    seq_lane = lax.broadcasted_iota(jnp.int32, (head_count, seq_acc.shape[1]), 1)

    def second_half(i):
        rows = block_rows(second_ranges[i])
        for c in range(n_chunks):
            cols = slice(c * chunk, (c + 1) * chunk)
            total = acc[rows, cols]
            for off in range(1, n_mp):
                total = total + jnp.dot(attn[off, rows, :], w[off, :, cols], preferred_element_type=jnp.float32)
            resid[rows, cols] = (hidden[rows, cols].astype(jnp.float32) + total).astype(jnp.bfloat16)

    def head_sums(i):
        rows = block_rows(head_ranges[i])
        count = rows.stop - rows.start
        out = lax.dot_general(
            heads_w[...], resid[rows, :], (((1,), (1,)), ((), ())), preferred_element_type=jnp.float32
        )
        part[0, 0:h, rows] = out[0:h] + out[h : 2 * h] + out[2 * h : 3 * h]
        squares = jnp.zeros((count, LANES), jnp.float32)
        for c in range(n_local // LANES):
            piece = resid[rows, c * LANES : (c + 1) * LANES].astype(jnp.float32)
            squares = squares + piece * piece
        sum_row = jnp.sum(jnp.transpose(squares), axis=0, keepdims=True)
        part[0, h : 2 * h, rows] = jnp.broadcast_to(sum_row, (h, count))

    def send_heads(i):
        for off in range(1, n_mp):
            part_copy(off, i).start()

    with jax.named_scope("otherw"):
        other_w("wait")
    for i in range(len(second_ranges)):
        with jax.named_scope("attnw"):
            hid_copy(i).wait()
            for off in range(1, n_mp):
                attn_copy(off, i).wait()
        second_half(i)
        if i > 0:
            head_sums(i - 1)
            send_heads(i - 1)
    with jax.named_scope("heads"):
        head_sums(len(head_ranges) - 1)
        send_heads(len(head_ranges) - 1)

    with jax.named_scope("gap"):
        for copy in small[2:]:
            copy.wait()
        all_slots = seq_s.shape[0]
        slot_lane = lax.broadcasted_iota(jnp.int32, (1, all_slots), 1)
        seq_row = seq_v[...].reshape(1, all_slots)
        token = lax.broadcasted_iota(jnp.int32, (1, block_len), 1).astype(jnp.float32)
        for j in range(slots):
            seq = seq_s[base + j]
            earlier = jnp.where((seq_row == seq) & (slot_lane < base + j), 1.0, 0.0)
            rank = jnp.sum(earlier, axis=1, keepdims=True)
            length = len_s[jnp.maximum(seq, 0)].astype(jnp.float32)
            valid = length - rank * float(block_len)
            live[j : j + 1, :] = jnp.where(token < valid, 1.0, 0.0)

    def own_at(m):
        return m if n_mp == 2 else lax.rem(m + n_mp - mp, n_mp)

    def finish(i):
        rows = block_rows(head_ranges[i])
        for off in range(1, n_mp):
            part_copy(off, i).wait()
        total = part[own_at(0), :, rows]
        for m in range(1, n_mp):
            total = total + part[own_at(m), :, rows]
        scale = lax.rsqrt(total[head_count:] / model_width + norm_epsilon)
        values = total[:head_count] * scale
        for b, j in enumerate(range(*head_ranges[i])):
            block = values[:, b * block_len : (b + 1) * block_len] * live[pl.ds(j, 1), :]
            rewards[j] = block
            sums = jnp.sum(block, axis=1, keepdims=True)
            seq_acc[...] += jnp.where(seq_lane == seq_s[base + j], sums, 0.0)

    with jax.named_scope("fin0"):
        for i in range(len(head_ranges) - 1):
            finish(i)
    def send_body(r, carry):
        low_dest = r * OWN_CAP
        found = jnp.int32(0)
        for j in range(slots):
            d = dest_s[base + j]
            found = jnp.where((d >= low_dest) & (d < low_dest + OWN_CAP), jnp.int32(j), found)
        send_idx[r] = found
        return carry

    with jax.named_scope("sidx"):
        lax.fori_loop(0, n_dp, send_body, 0)
    with jax.named_scope("finl"):
        finish(len(head_ranges) - 1)
    for k in range(n_dp - 1, 0, -1):
        sum_copy(k).start()

    def fill(r, carry):
        send_buf[r] = rewards[send_idx[r]]
        return carry

    lax.fori_loop(0, n_dp, fill, 0, unroll=n_dp <= 16)
    for k in range(n_dp - 1, 0, -1):
        rew_copy(k).start()
    recv_sum[dp] = seq_acc[...]
    recv_rew[dp] = rewards[send_idx[dp]]
    dest_row = dest_v[...].reshape(1, all_slots)
    sources = []
    for q in range(OWN_CAP):
        place = jnp.max(jnp.where(dest_row == dp * OWN_CAP + q, slot_lane, 0))
        sources.append(lax.div(place, slots))
    lengths_row = len_v[...].reshape(1, seq_count).astype(jnp.float32)

    with jax.named_scope("sumw"):
        wait_all(recv_sum, sum_send)
        wait_all(recv_sum, sum_recv)
    totals = recv_sum[0]
    for s in range(1, n_dp):
        totals = totals + recv_sum[s]
    scores = totals[:, :seq_count] / lengths_row
    worst = jnp.min(scores, axis=0, keepdims=True)
    centred = scores - jnp.mean(scores, axis=0, keepdims=True)
    spread = jnp.mean(centred * centred, axis=0, keepdims=True)
    penalty_scale = jnp.mean(spread, axis=1, keepdims=True) + stat_epsilon
    conservative = worst - spread / penalty_scale
    shifted = conservative - jnp.mean(conservative, axis=1, keepdims=True)
    variance = jnp.mean(shifted * shifted, axis=1, keepdims=True)
    adv_buf[...] = jnp.zeros_like(adv_buf)
    adv_buf[0:1, :seq_count] = shifted * lax.rsqrt(variance + stat_epsilon)
    width = adv_buf.shape[1]
    seq_local = adv_out.shape[1]
    turned = pltpu.roll(adv_buf[...], width - dp * seq_local, 1)
    adv_out[...] = turned[0:1, :seq_local]
    with jax.named_scope("reww"):
        wait_all(recv_rew, rew_send)
        wait_all(recv_rew, rew_recv)
    with jax.named_scope("outs"):
        for q in range(OWN_CAP):
            rewards_out[q] = recv_rew[sources[q]]


def store_kernel(rewards_ref, adv_ref, rewards_hbm, adv_hbm, sems):
    copies = [
        pltpu.make_async_copy(rewards_ref, rewards_hbm, sems.at[0]),
        pltpu.make_async_copy(adv_ref, adv_hbm, sems.at[1]),
    ]
    for copy in copies:
        copy.start()
    for copy in copies:
        copy.wait()


def local(n_dp, n_mp, hidden, attn_out, out_proj, norm_gain, reward_proj, block_seq, block_dest, lengths):
    slots, block_len, k_local = attn_out.shape
    n_local = out_proj.shape[1]
    seq_count = lengths.shape[0]
    seq_pad = -(-seq_count // LANES) * LANES
    heads = reward_proj.shape[1]
    groups = split_slots(slots)
    n_first, n_second, n_heads = map(len, groups)
    total_rows = slots * block_len
    f32, bf16 = jnp.float32, jnp.bfloat16
    dma = pltpu.SemaphoreType.DMA
    any_spec = pl.BlockSpec(memory_space=pl.ANY)
    vmem_spec = pl.BlockSpec(memory_space=pltpu.VMEM)
    in_hbm = functools.partial(pltpu.with_memory_space_constraint, memory_space=pltpu.HBM)
    in_vmem = functools.partial(pltpu.with_memory_space_constraint, memory_space=pltpu.VMEM)
    rewards_shape = (OWN_CAP, heads, block_len)
    adv_shape = (1, seq_count // n_dp)
    results = pl.pallas_call(
        functools.partial(kernel, n_dp, n_mp, slots, block_len, seq_count, groups),
        out_shape=(pltpu.VMEM(rewards_shape, f32), pltpu.VMEM(adv_shape, f32)),
        in_specs=[any_spec] * 8,
        out_specs=(vmem_spec, vmem_spec),
        scratch_shapes=[
            pltpu.VMEM((n_mp, total_rows, k_local), bf16),
            pltpu.VMEM((n_mp, k_local, n_local), bf16),
            pltpu.VMEM((total_rows, n_local), bf16),
            pltpu.VMEM((total_rows, n_local), f32),
            pltpu.VMEM((total_rows, n_local), bf16),
            pltpu.VMEM((4 * heads, n_local), bf16),
            pltpu.VMEM((n_mp, 2 * heads, total_rows), f32),
            pltpu.VMEM((slots + (-slots) % 8, block_len), f32),
            pltpu.VMEM((slots, heads, block_len), f32),
            pltpu.VMEM((heads, seq_pad), f32),
            pltpu.VMEM((n_dp, heads, block_len), f32),
            pltpu.VMEM((n_dp, heads, seq_pad), f32),
            pltpu.VMEM((n_dp, heads, block_len), f32),
            pltpu.VMEM((8, seq_pad), f32),
            pltpu.SMEM((n_dp,), jnp.int32),
            pltpu.VMEM(norm_gain.shape, f32),
            pltpu.VMEM((heads, n_local), f32),
            pltpu.SMEM(block_seq.shape, jnp.int32),
            pltpu.SMEM(block_dest.shape, jnp.int32),
            pltpu.SMEM(lengths.shape, jnp.int32),
            pltpu.VMEM(block_seq.shape, jnp.int32),
            pltpu.VMEM(block_dest.shape, jnp.int32),
            pltpu.VMEM(lengths.shape, jnp.int32),
            dma((8,)),
            dma((n_mp, 2)),
            dma((n_first + 1,)),
            dma((n_second,)),
            dma((n_mp - 1, n_second)),
            dma((n_mp - 1, n_second)),
            dma((n_mp - 1, n_heads)),
            dma((n_mp - 1, n_heads)),
            *[dma] * 4,
        ],
        compiler_params=pltpu.CompilerParams(
            collective_id=0, has_side_effects=True, vmem_limit_bytes=40 * 1024 * 1024
        ),
    )(
        in_hbm(hidden.reshape(total_rows, n_local)),
        in_hbm(attn_out.reshape(total_rows, k_local)),
        in_hbm(out_proj),
        in_hbm(norm_gain),
        in_hbm(reward_proj.T),
        in_hbm(block_seq),
        in_hbm(block_dest),
        in_hbm(lengths),
    )
    token_rewards, advantages = pl.pallas_call(
        store_kernel,
        out_shape=(jax.ShapeDtypeStruct(rewards_shape, f32), jax.ShapeDtypeStruct(adv_shape, f32)),
        in_specs=[vmem_spec] * 2,
        out_specs=(any_spec, any_spec),
        scratch_shapes=[dma((2,))],
    )(*map(in_vmem, results))
    return token_rewards, advantages.reshape(seq_count // n_dp)


def solution(mesh):
    return jax.shard_map(
        functools.partial(local, mesh.shape["dp"], mesh.shape["mp"]),
        mesh=mesh,
        in_specs=(
            P("dp", None, "mp"),
            P("dp", None, "mp"),
            P(None, "mp"),
            P("mp"),
            P("mp", None),
            P(),
            P(),
            P(),
        ),
        out_specs=(P("dp", None, None), P("dp")),
        check_vma=False,
    )
```

time: 26.9 us -> 25.2 us (0.937)
  Pallas kernels: 26.1 us -> 24.4 us
    pallas_call x1, Pallas kernels: 1.89 us -> 0.64 us  [local(): pl.pallas_call(store_kernel, out_shape=(jax.ShapeDtypeStruct(rewards_shap...]
    pallas_call x1, Pallas kernels: 24.2 us -> 23.7 us  [local(): pl.pallas_call(functools.partial(kernel, n_dp, n_mp, slots, block_len, se...]
where the time goes in v1:
time: 25.2 us; the launch traced here: 25 us
  Pallas kernels  24.4 us (97%)
  between operations  0.64 us (3%)
    pallas_call x1, Pallas kernels, local(): pl.pallas_call(functools.partial(kernel, n_dp, n_mp, slots, block_len, se...  23.7 us
    pallas_call x1, Pallas kernels, local(): pl.pallas_call(store_kernel, out_shape=(jax.ShapeDtypeStruct(rewards_shap...  0.64 us

profile of v1, /device:TPU:0, one launch (start us, length us, event | category | flops | bytes accessed | tf_op | source)
XLA Modules:
  0.0 25.0 jit_solution(823444629252957369)
XLA Ops:
  0.6 23.7 %shard_map.95 = (f32[10,8,128]{2,1,0:T(8,128)S(1)}, f32[1,6]{1,0:T(1,128)S(1)}) custom-call(bf16[1920,1024]{1,0:T(8,128)(2,1)} %bitcast.4, bf16[1920,1024]{1,0:T(8,128)(2,1)} %bitcast.5, bf16[2048,1024]{1,0:T(8,128)(2,1)} %w_hbm.1, f32[1024]{0:T(1024)} %gain_hbm.1, f32[8,1024]{1,0:T(8,128)} %bitcast.6, s32[240]{0:T(256)} %seq_hbm.1, s32[240]{0:T(256)} %dest_hbm.1, ...), custom_call_target="tpu_custom_call" | custom-call | tf_op jit(solution)/shard_map/pallas_call | solution.py:386
  24.4 0.6 %shard_map.96 = (f32[10,8,128]{2,1,0:T(8,128)}, f32[1,6]{1,0:T(1,128)}) custom-call(f32[10,8,128]{2,1,0:T(8,128)S(1)} %get-tuple-element.6.rewards_ref, f32[1,6]{1,0:T(1,128)S(1)} %get-tuple-element.7.adv_ref), custom_call_target="tpu_custom_call" | custom-call | tf_op jit(solution)/shard_map/pallas_call | solution.py:438

commit v2 on v1

v2 whole, which is shorter than its diff:
```python
import functools

import jax
import jax.numpy as jnp
from jax import lax
from jax.experimental import pallas as pl
from jax.experimental.pallas import tpu as pltpu
from jax.sharding import PartitionSpec as P

OWN_CAP = 10

norm_epsilon = 1e-05
stat_epsilon = 1e-06
MESH = pl.DeviceIdType.MESH
LANES = 128


def split_size(slots):
    for size in (5, 4, 3, 2):
        if slots % size == 0:
            return size
    return 1


def partner(index, k, n):
    if n & (n - 1):
        return lax.rem(index + k, n)
    out = index
    bit = 1
    while bit < n:
        if k & bit:
            out = out + bit - 2 * bit * lax.rem(lax.div(index, bit), 2)
        bit *= 2
    return out


def kernel(
    n_dp, n_mp, slots, block_len, seq_count, per_group,
    hidden_hbm, attn_hbm, w_hbm, gain_hbm, reward_hbm, seq_hbm, dest_hbm, len_hbm,
    rewards_out, adv_out,
    attn, w, hidden, acc, resid, heads_w, part, live, rewards, seq_acc, send_buf,
    recv_sum, recv_rew, adv_buf,
    send_idx, gain_ref, reward_ref, seq_s, dest_s, len_s, seq_v, dest_v, len_v, small_sem,
    w_sem, own_sem, hid_sem, attn_send, attn_recv, part_send, part_recv,
    sum_send, sum_recv, rew_send, rew_recv,
):
    dp = lax.axis_index("dp")
    mp = lax.axis_index("mp")
    n_groups = slots // per_group
    rows = per_group * block_len
    k_local = attn_hbm.shape[1]
    n_local = w_hbm.shape[1]
    model_width = w_hbm.shape[0]
    chunk = min(256, n_local)
    n_chunks = n_local // chunk
    head_count = reward_ref.shape[0]
    h = head_count
    base = dp * slots

    barrier = pltpu.get_barrier_semaphore()
    for off in range(1, n_mp):
        pl.semaphore_signal(barrier, inc=1, device_id=(dp, lax.rem(mp + off, n_mp)), device_id_type=MESH)
    across = lax.rem(mp + 1, n_mp) if n_mp == 2 else mp
    for k in range(n_dp - 1, 0, -1):
        pl.semaphore_signal(barrier, inc=1, device_id=(partner(dp, k, n_dp), across), device_id_type=MESH)

    def group_rows(g):
        return pl.ds(pl.multiple_of(g * rows, rows), rows)

    lead_rows, rest_rows = slice(0, rows), slice(rows, slots * block_len)

    k_half = k_local // 2

    def w_copy(off, half):
        start = pl.multiple_of(lax.rem(mp + off, n_mp) * k_local + half * k_half, k_half)
        return pltpu.make_async_copy(
            w_hbm.at[pl.ds(start, k_half)], w.at[off, half * k_half : (half + 1) * k_half], w_sem.at[off, half]
        )

    def lead_copy(half):
        cols = slice(half * k_half, (half + 1) * k_half)
        return pltpu.make_async_copy(attn_hbm.at[lead_rows, cols], attn.at[0, lead_rows, cols], own_sem.at[half])

    def rest_copy():
        return pltpu.make_async_copy(attn_hbm.at[rest_rows], attn.at[0, rest_rows], own_sem.at[2])

    def other_w(action):
        for off in range(1, n_mp):
            for half in range(2):
                getattr(w_copy(off, half), action)()

    def hid_copy():
        return pltpu.make_async_copy(hidden_hbm, hidden, hid_sem)

    def attn_copy(off, g):
        return pltpu.make_async_remote_copy(
            src_ref=attn_hbm.at[group_rows(g)],
            dst_ref=attn.at[n_mp - off, group_rows(g)],
            send_sem=attn_send.at[off - 1, g],
            recv_sem=attn_recv.at[off - 1, g],
            device_id=(dp, lax.rem(mp + off, n_mp)),
            device_id_type=MESH,
        )

    def part_copy(off, g):
        return pltpu.make_async_remote_copy(
            src_ref=part.at[0, g],
            dst_ref=part.at[n_mp - off, g],
            send_sem=part_send.at[off - 1, g],
            recv_sem=part_recv.at[off - 1, g],
            device_id=(dp, lax.rem(mp + off, n_mp)),
            device_id_type=MESH,
        )

    def sum_copy(k):
        return pltpu.make_async_remote_copy(
            src_ref=seq_acc,
            dst_ref=recv_sum.at[dp],
            send_sem=sum_send,
            recv_sem=sum_recv,
            device_id=(partner(dp, k, n_dp), across),
            device_id_type=MESH,
        )

    def rew_copy(k):
        peer = partner(dp, k, n_dp)
        return pltpu.make_async_remote_copy(
            src_ref=send_buf.at[peer],
            dst_ref=recv_rew.at[dp],
            send_sem=rew_send,
            recv_sem=rew_recv,
            device_id=(peer, across),
            device_id_type=MESH,
        )

    def wait_all(ref, sem):
        others = ref.at[0 : n_dp - 1]
        pltpu.make_async_copy(others, others, sem).wait()

    w_copy(0, 0).start()
    lead_copy(0).start()
    small = [
        pltpu.make_async_copy(src, dst, small_sem.at[i])
        for i, (src, dst) in enumerate(
            (
                (gain_hbm, gain_ref),
                (reward_hbm, reward_ref),
                (dest_hbm, dest_s),
                (seq_hbm, seq_s),
                (len_hbm, len_s),
                (seq_hbm, seq_v),
                (dest_hbm, dest_v),
                (len_hbm, len_v),
            )
        )
    ]
    for copy in small:
        copy.start()
    w_copy(0, 1).start(priority=1)
    lead_copy(1).start(priority=1)
    if n_groups > 1:
        rest_copy().start(priority=1)
    with jax.named_scope("smallw"):
        small[0].wait()
        small[1].wait()
    weighted = reward_ref[...] * gain_ref[...].reshape(1, n_local)
    high = weighted.astype(jnp.bfloat16)
    rest = weighted - high.astype(jnp.float32)
    middle = rest.astype(jnp.bfloat16)
    low = (rest - middle.astype(jnp.float32)).astype(jnp.bfloat16)
    heads_w[...] = jnp.concatenate([high, middle, low, jnp.zeros_like(low)], axis=0)
    seq_acc[...] = jnp.zeros_like(seq_acc)

    def lead(half):
        depth = slice(half * k_half, (half + 1) * k_half)
        for c in range(n_chunks):
            cols = slice(c * chunk, (c + 1) * chunk)
            product = jnp.dot(attn[0, lead_rows, depth], w[0, depth, cols], preferred_element_type=jnp.float32)
            acc[lead_rows, cols] = acc[lead_rows, cols] + product if half else product

    def send_attn(i):
        if i < n_groups:
            for off in range(1, n_mp):
                attn_copy(off, i).start()

    with jax.named_scope("sidxw"):
        small[2].wait()
    def send_body(r, carry):
        low_dest = r * OWN_CAP
        found = jnp.int32(0)
        for j in range(slots):
            d = dest_s[base + j]
            found = jnp.where((d >= low_dest) & (d < low_dest + OWN_CAP), jnp.int32(j), found)
        send_idx[r] = found
        return carry

    with jax.named_scope("sidx"):
        lax.fori_loop(0, n_dp, send_body, 0)
    with jax.named_scope("lead0"):
        w_copy(0, 0).wait()
        lead_copy(0).wait()
    lead(0)
    with jax.named_scope("barr"):
        pl.semaphore_wait(barrier, n_mp - 1 + n_dp - 1)
    send_attn(0)
    with jax.named_scope("lead1"):
        w_copy(0, 1).wait()
        lead_copy(1).wait()
    lead(1)
    send_attn(1)
    if n_groups > 1:
        with jax.named_scope("ownw"):
            rest_copy().wait()
    other_w("start")
    hid_copy().start()
    if n_groups > 1:
        for c in range(n_chunks):
            cols = slice(c * chunk, (c + 1) * chunk)
            acc[rest_rows, cols] = jnp.dot(
                attn[0, rest_rows, :], w[0, :, cols], preferred_element_type=jnp.float32
            )
    for g in range(2, n_groups):
        send_attn(g)

    seq_lane = lax.broadcasted_iota(jnp.int32, (head_count, seq_acc.shape[1]), 1)

    def second_half(g, carry):
        with jax.named_scope("attnw"):
            for off in range(1, n_mp):
                attn_copy(off, g).wait_recv()
        squares = jnp.zeros((rows, LANES), jnp.float32)
        for c in range(n_chunks):
            cols = slice(c * chunk, (c + 1) * chunk)
            total = acc[group_rows(g), cols]
            for off in range(1, n_mp):
                total = total + jnp.dot(
                    attn[off, group_rows(g), :], w[off, :, cols], preferred_element_type=jnp.float32
                )
            stored = (hidden[group_rows(g), cols].astype(jnp.float32) + total).astype(jnp.bfloat16)
            resid[:, cols] = stored
            v = stored.astype(jnp.float32)
            for i in range(chunk // LANES):
                piece = v[:, i * LANES : (i + 1) * LANES]
                squares = squares + piece * piece
        out = lax.dot_general(
            heads_w[...], resid[...], (((1,), (1,)), ((), ())), preferred_element_type=jnp.float32
        )
        part[0, g, 0:h, :] = out[0:h] + out[h : 2 * h] + out[2 * h : 3 * h]
        sum_row = jnp.sum(jnp.transpose(squares), axis=0, keepdims=True)
        part[0, g, h : 2 * h, :] = jnp.broadcast_to(sum_row, (h, rows))
        for off in range(1, n_mp):
            part_copy(off, g).start()
        return carry

    with jax.named_scope("otherw"):
        other_w("wait")
        hid_copy().wait()
    lax.fori_loop(0, n_groups, second_half, 0)

    with jax.named_scope("gap"):
        for copy in small[3:]:
            copy.wait()
        all_slots = seq_s.shape[0]
        slot_lane = lax.broadcasted_iota(jnp.int32, (1, all_slots), 1)
        seq_row = seq_v[...].reshape(1, all_slots)
        token = lax.broadcasted_iota(jnp.int32, (1, block_len), 1).astype(jnp.float32)
        for j in range(slots):
            seq = seq_s[base + j]
            earlier = jnp.where((seq_row == seq) & (slot_lane < base + j), 1.0, 0.0)
            rank = jnp.sum(earlier, axis=1, keepdims=True)
            length = len_s[jnp.maximum(seq, 0)].astype(jnp.float32)
            valid = length - rank * float(block_len)
            live[j : j + 1, :] = jnp.where(token < valid, 1.0, 0.0)

    def own_at(m):
        return m if n_mp == 2 else lax.rem(m + n_mp - mp, n_mp)

    def finish(g):
        for off in range(1, n_mp):
            part_copy(off, g).wait_recv()
        total = part[own_at(0), g]
        for m in range(1, n_mp):
            total = total + part[own_at(m), g]
        scale = lax.rsqrt(total[h:] / model_width + norm_epsilon)
        values = total[:h] * scale
        for b in range(per_group):
            j = g * per_group + b
            block = values[:, b * block_len : (b + 1) * block_len] * live[pl.ds(j, 1), :]
            rewards[j] = block
            sums = jnp.sum(block, axis=1, keepdims=True)
            seq_acc[...] += jnp.where(seq_lane == seq_s[base + j], sums, 0.0)

    with jax.named_scope("fin0"):
        for g in range(n_groups - 1):
            finish(g)
    with jax.named_scope("finl"):
        finish(n_groups - 1)
    for k in range(n_dp - 1, 0, -1):
        sum_copy(k).start()

    def fill(r, carry):
        send_buf[r] = rewards[send_idx[r]].astype(send_buf.dtype)
        return carry

    lax.fori_loop(0, n_dp, fill, 0, unroll=n_dp <= 16)
    for k in range(n_dp - 1, 0, -1):
        rew_copy(k).start()
    recv_sum[dp] = seq_acc[...]
    recv_rew[dp] = rewards[send_idx[dp]].astype(recv_rew.dtype)
    dest_row = dest_v[...].reshape(1, all_slots)
    sources = []
    for q in range(OWN_CAP):
        place = jnp.max(jnp.where(dest_row == dp * OWN_CAP + q, slot_lane, 0))
        sources.append(lax.div(place, slots))
    lengths_row = len_v[...].reshape(1, seq_count).astype(jnp.float32)

    with jax.named_scope("sumw"):
        wait_all(recv_sum, sum_recv)
    totals = recv_sum[0]
    for s in range(1, n_dp):
        totals = totals + recv_sum[s]
    scores = totals[:, :seq_count] / lengths_row
    worst = jnp.min(scores, axis=0, keepdims=True)
    centred = scores - jnp.mean(scores, axis=0, keepdims=True)
    spread = jnp.mean(centred * centred, axis=0, keepdims=True)
    spread_mean = jnp.mean(spread, axis=1, keepdims=True)
    worst_mean = jnp.mean(worst, axis=1, keepdims=True)
    penalty_scale = spread_mean + stat_epsilon
    shifted = (worst - spread / penalty_scale) - (worst_mean - spread_mean / penalty_scale)
    variance = jnp.mean(shifted * shifted, axis=1, keepdims=True)
    adv_buf[...] = jnp.zeros_like(adv_buf)
    adv_buf[0:1, :seq_count] = shifted * lax.rsqrt(variance + stat_epsilon)
    width = adv_buf.shape[1]
    seq_local = adv_out.shape[1]
    turned = pltpu.roll(adv_buf[...], width - dp * seq_local, 1)
    adv_out[...] = turned[0:1, :seq_local]
    with jax.named_scope("reww"):
        wait_all(recv_rew, rew_recv)
    with jax.named_scope("outs"):
        for q in range(OWN_CAP):
            rewards_out[q] = recv_rew[sources[q]].astype(jnp.float32)
    with jax.named_scope("sends"):
        for off in range(1, n_mp):
            for g in range(n_groups):
                part_copy(off, g).wait_send()
                attn_copy(off, g).wait_send()
        wait_all(recv_sum, sum_send)
        wait_all(recv_rew, rew_send)


def store_kernel(rewards_ref, adv_ref, rewards_hbm, adv_hbm, sems):
    copies = [
        pltpu.make_async_copy(rewards_ref, rewards_hbm, sems.at[0]),
        pltpu.make_async_copy(adv_ref, adv_hbm, sems.at[1]),
    ]
    for copy in copies:
        copy.start()
    for copy in copies:
        copy.wait()


REW = jnp.bfloat16


def local(n_dp, n_mp, hidden, attn_out, out_proj, norm_gain, reward_proj, block_seq, block_dest, lengths):
    slots, block_len, k_local = attn_out.shape
    n_local = out_proj.shape[1]
    seq_count = lengths.shape[0]
    seq_pad = -(-seq_count // LANES) * LANES
    heads = reward_proj.shape[1]
    per_group = split_size(slots)
    n_groups = slots // per_group
    rows = per_group * block_len
    total_rows = slots * block_len
    f32, bf16 = jnp.float32, jnp.bfloat16
    dma = pltpu.SemaphoreType.DMA
    any_spec = pl.BlockSpec(memory_space=pl.ANY)
    vmem_spec = pl.BlockSpec(memory_space=pltpu.VMEM)
    in_hbm = functools.partial(pltpu.with_memory_space_constraint, memory_space=pltpu.HBM)
    in_vmem = functools.partial(pltpu.with_memory_space_constraint, memory_space=pltpu.VMEM)
    rewards_shape = (OWN_CAP, heads, block_len)
    adv_shape = (1, seq_count // n_dp)
    results = pl.pallas_call(
        functools.partial(kernel, n_dp, n_mp, slots, block_len, seq_count, per_group),
        out_shape=(pltpu.VMEM(rewards_shape, f32), pltpu.VMEM(adv_shape, f32)),
        in_specs=[any_spec] * 8,
        out_specs=(vmem_spec, vmem_spec),
        scratch_shapes=[
            pltpu.VMEM((n_mp, total_rows, k_local), bf16),
            pltpu.VMEM((n_mp, k_local, n_local), bf16),
            pltpu.VMEM((total_rows, n_local), bf16),
            pltpu.VMEM((total_rows, n_local), f32),
            pltpu.VMEM((rows, n_local), bf16),
            pltpu.VMEM((4 * heads, n_local), bf16),
            pltpu.VMEM((n_mp, n_groups, 2 * heads, rows), f32),
            pltpu.VMEM((slots + (-slots) % 8, block_len), f32),
            pltpu.VMEM((slots, heads, block_len), f32),
            pltpu.VMEM((heads, seq_pad), f32),
            pltpu.VMEM((n_dp, heads, block_len), REW),
            pltpu.VMEM((n_dp, heads, seq_pad), f32),
            pltpu.VMEM((n_dp, heads, block_len), REW),
            pltpu.VMEM((8, seq_pad), f32),
            pltpu.SMEM((n_dp,), jnp.int32),
            pltpu.VMEM(norm_gain.shape, f32),
            pltpu.VMEM((heads, n_local), f32),
            pltpu.SMEM(block_seq.shape, jnp.int32),
            pltpu.SMEM(block_dest.shape, jnp.int32),
            pltpu.SMEM(lengths.shape, jnp.int32),
            pltpu.VMEM(block_seq.shape, jnp.int32),
            pltpu.VMEM(block_dest.shape, jnp.int32),
            pltpu.VMEM(lengths.shape, jnp.int32),
            dma((8,)),
            dma((n_mp, 2)),
            dma((3,)),
            dma,
            dma((n_mp - 1, n_groups)),
            dma((n_mp - 1, n_groups)),
            dma((n_mp - 1, n_groups)),
            dma((n_mp - 1, n_groups)),
            *[dma] * 4,
        ],
        compiler_params=pltpu.CompilerParams(
            collective_id=0, has_side_effects=True, vmem_limit_bytes=40 * 1024 * 1024
        ),
    )(
        in_hbm(hidden.reshape(total_rows, n_local)),
        in_hbm(attn_out.reshape(total_rows, k_local)),
        in_hbm(out_proj),
        in_hbm(norm_gain),
        in_hbm(reward_proj.T),
        in_hbm(block_seq),
        in_hbm(block_dest),
        in_hbm(lengths),
    )
    token_rewards, advantages = pl.pallas_call(
        store_kernel,
        out_shape=(jax.ShapeDtypeStruct(rewards_shape, f32), jax.ShapeDtypeStruct(adv_shape, f32)),
        in_specs=[vmem_spec] * 2,
        out_specs=(any_spec, any_spec),
        scratch_shapes=[dma((2,))],
    )(*map(in_vmem, results))
    return token_rewards, advantages.reshape(seq_count // n_dp)


def solution(mesh):
    return jax.shard_map(
        functools.partial(local, mesh.shape["dp"], mesh.shape["mp"]),
        mesh=mesh,
        in_specs=(
            P("dp", None, "mp"),
            P("dp", None, "mp"),
            P(None, "mp"),
            P("mp"),
            P("mp", None),
            P(),
            P(),
            P(),
        ),
        out_specs=(P("dp", None, None), P("dp")),
        check_vma=False,
    )
```

time: 25.2 us -> 23.7 us (0.940)
  Pallas kernels: 24.4 us -> 22.9 us
    pallas_call x1, Pallas kernels: 23.7 us -> 22.3 us  [local(): pl.pallas_call(functools.partial(kernel, n_dp, n_mp, slots, block_len, se...]
where the time goes in v2:
time: 23.7 us; the launch traced here: 23.5 us
  Pallas kernels  22.9 us (97%)
  between operations  0.64 us (3%)
    pallas_call x1, Pallas kernels, local(): pl.pallas_call(functools.partial(kernel, n_dp, n_mp, slots, block_len, se...  22.3 us
    pallas_call x1, Pallas kernels, local(): pl.pallas_call(store_kernel, out_shape=(jax.ShapeDtypeStruct(rewards_shap...  0.64 us

profile of v2, /device:TPU:0, one launch (start us, length us, event | category | flops | bytes accessed | tf_op | source)
XLA Modules:
  0.0 23.5 jit_solution(4967324989276945824)
XLA Ops:
  0.6 22.3 %shard_map.95 = (f32[10,8,128]{2,1,0:T(8,128)S(1)}, f32[1,6]{1,0:T(1,128)S(1)}) custom-call(bf16[1920,1024]{1,0:T(8,128)(2,1)} %bitcast.4, bf16[1920,1024]{1,0:T(8,128)(2,1)} %bitcast.5, bf16[2048,1024]{1,0:T(8,128)(2,1)} %w_hbm.1, f32[1024]{0:T(1024)} %gain_hbm.1, f32[8,1024]{1,0:T(8,128)} %bitcast.6, s32[240]{0:T(256)} %seq_hbm.1, s32[240]{0:T(256)} %dest_hbm.1, ...), custom_call_target="tpu_custom_call" | custom-call | tf_op jit(solution)/shard_map/pallas_call | solution.py:383
  22.9 0.6 %shard_map.96 = (f32[10,8,128]{2,1,0:T(8,128)}, f32[1,6]{1,0:T(1,128)}) custom-call(f32[10,8,128]{2,1,0:T(8,128)S(1)} %get-tuple-element.6.rewards_ref, f32[1,6]{1,0:T(1,128)S(1)} %get-tuple-element.7.adv_ref), custom_call_target="tpu_custom_call" | custom-call | tf_op jit(solution)/shard_map/pallas_call | solution.py:435

commit v3 on v2

--- a/solution.py
+++ b/solution.py
@@ -38,9 +38,9 @@
     n_dp, n_mp, slots, block_len, seq_count, per_group,
     hidden_hbm, attn_hbm, w_hbm, gain_hbm, reward_hbm, seq_hbm, dest_hbm, len_hbm,
     rewards_out, adv_out,
-    attn, w, hidden, acc, resid, heads_w, part, live, rewards, seq_acc, send_buf,
+    attn, w, hidden, acc, resid, heads_w, part, live, rewards, seq_acc, sum_row, send_buf,
     recv_sum, recv_rew, adv_buf,
-    send_idx, gain_ref, reward_ref, seq_s, dest_s, len_s, seq_v, dest_v, len_v, small_sem,
+    send_idx, gain_ref, reward_ref, seq_s, len_s, seq_v, dest_v, len_v, small_sem,
     w_sem, own_sem, hid_sem, attn_send, attn_recv, part_send, part_recv,
     sum_send, sum_recv, rew_send, rew_recv,
 ):
@@ -69,25 +69,28 @@
 
     lead_rows, rest_rows = slice(0, rows), slice(rows, slots * block_len)
 
-    k_half = k_local // 2
-
-    def w_copy(off, half):
-        start = pl.multiple_of(lax.rem(mp + off, n_mp) * k_local + half * k_half, k_half)
+    depths = (slice(0, k_local // LEAD), slice(k_local // LEAD, k_local))
+
+    def w_copy(off, part_at):
+        depth = depths[part_at]
+        start = pl.multiple_of(lax.rem(mp + off, n_mp) * k_local + depth.start, LANES)
         return pltpu.make_async_copy(
-            w_hbm.at[pl.ds(start, k_half)], w.at[off, half * k_half : (half + 1) * k_half], w_sem.at[off, half]
-        )
-
-    def lead_copy(half):
-        cols = slice(half * k_half, (half + 1) * k_half)
-        return pltpu.make_async_copy(attn_hbm.at[lead_rows, cols], attn.at[0, lead_rows, cols], own_sem.at[half])
+            w_hbm.at[pl.ds(start, depth.stop - depth.start)], w.at[off, depth], w_sem.at[off, part_at]
+        )
+
+    def lead_copy(part_at):
+        depth = depths[part_at]
+        return pltpu.make_async_copy(
+            attn_hbm.at[lead_rows, depth], attn.at[0, lead_rows, depth], own_sem.at[part_at]
+        )
 
     def rest_copy():
         return pltpu.make_async_copy(attn_hbm.at[rest_rows], attn.at[0, rest_rows], own_sem.at[2])
 
     def other_w(action):
         for off in range(1, n_mp):
-            for half in range(2):
-                getattr(w_copy(off, half), action)()
+            for i in range(len(depths)):
+                getattr(w_copy(off, i), action)()
 
     def hid_copy():
         return pltpu.make_async_copy(hidden_hbm, hidden, hid_sem)
@@ -96,7 +99,7 @@
         return pltpu.make_async_remote_copy(
             src_ref=attn_hbm.at[group_rows(g)],
             dst_ref=attn.at[n_mp - off, group_rows(g)],
-            send_sem=attn_send.at[off - 1, g],
+            send_sem=attn_send.at[off - 1],
             recv_sem=attn_recv.at[off - 1, g],
             device_id=(dp, lax.rem(mp + off, n_mp)),
             device_id_type=MESH,
@@ -106,7 +109,7 @@
         return pltpu.make_async_remote_copy(
             src_ref=part.at[0, g],
             dst_ref=part.at[n_mp - off, g],
-            send_sem=part_send.at[off - 1, g],
+            send_sem=part_send.at[off - 1],
             recv_sem=part_recv.at[off - 1, g],
             device_id=(dp, lax.rem(mp + off, n_mp)),
             device_id_type=MESH,
@@ -114,7 +117,7 @@
 
     def sum_copy(k):
         return pltpu.make_async_remote_copy(
-            src_ref=seq_acc,
+            src_ref=sum_row,
             dst_ref=recv_sum.at[dp],
             send_sem=sum_send,
             recv_sem=sum_recv,
@@ -145,11 +148,10 @@
             (
                 (gain_hbm, gain_ref),
                 (reward_hbm, reward_ref),
-                (dest_hbm, dest_s),
+                (dest_hbm, dest_v),
                 (seq_hbm, seq_s),
                 (len_hbm, len_s),
                 (seq_hbm, seq_v),
-                (dest_hbm, dest_v),
                 (len_hbm, len_v),
             )
         )
@@ -171,12 +173,12 @@
     heads_w[...] = jnp.concatenate([high, middle, low, jnp.zeros_like(low)], axis=0)
     seq_acc[...] = jnp.zeros_like(seq_acc)
 
-    def lead(half):
-        depth = slice(half * k_half, (half + 1) * k_half)
+    def lead(part_at):
+        depth = depths[part_at]
         for c in range(n_chunks):
             cols = slice(c * chunk, (c + 1) * chunk)
             product = jnp.dot(attn[0, lead_rows, depth], w[0, depth, cols], preferred_element_type=jnp.float32)
-            acc[lead_rows, cols] = acc[lead_rows, cols] + product if half else product
+            acc[lead_rows, cols] = acc[lead_rows, cols] + product if part_at else product
 
     def send_attn(i):
         if i < n_groups:
@@ -185,17 +187,14 @@
 
     with jax.named_scope("sidxw"):
         small[2].wait()
-    def send_body(r, carry):
-        low_dest = r * OWN_CAP
-        found = jnp.int32(0)
-        for j in range(slots):
-            d = dest_s[base + j]
-            found = jnp.where((d >= low_dest) & (d < low_dest + OWN_CAP), jnp.int32(j), found)
-        send_idx[r] = found
-        return carry
-
     with jax.named_scope("sidx"):
-        lax.fori_loop(0, n_dp, send_body, 0)
+        all_slots = dest_v.shape[0]
+        slot_lane = lax.broadcasted_iota(jnp.int32, (1, all_slots), 1)
+        dest_row = dest_v[...].reshape(1, all_slots)
+        own_dest = jnp.where((slot_lane >= base) & (slot_lane < base + slots), dest_row, -1)
+        for r in range(n_dp):
+            here = (own_dest >= r * OWN_CAP) & (own_dest < (r + 1) * OWN_CAP)
+            send_idx[r] = jnp.max(jnp.where(here, slot_lane - base, 0))
     with jax.named_scope("lead0"):
         w_copy(0, 0).wait()
         lead_copy(0).wait()
@@ -222,8 +221,6 @@
     for g in range(2, n_groups):
         send_attn(g)
 
-    seq_lane = lax.broadcasted_iota(jnp.int32, (head_count, seq_acc.shape[1]), 1)
-
     def second_half(g, carry):
         with jax.named_scope("attnw"):
             for off in range(1, n_mp):
@@ -246,8 +243,8 @@
             heads_w[...], resid[...], (((1,), (1,)), ((), ())), preferred_element_type=jnp.float32
         )
         part[0, g, 0:h, :] = out[0:h] + out[h : 2 * h] + out[2 * h : 3 * h]
-        sum_row = jnp.sum(jnp.transpose(squares), axis=0, keepdims=True)
-        part[0, g, h : 2 * h, :] = jnp.broadcast_to(sum_row, (h, rows))
+        square_row = jnp.sum(jnp.transpose(squares), axis=0, keepdims=True)
+        part[0, g, h : 2 * h, :] = jnp.broadcast_to(square_row, (h, rows))
         for off in range(1, n_mp):
             part_copy(off, g).start()
         return carry
@@ -260,8 +257,6 @@
     with jax.named_scope("gap"):
         for copy in small[3:]:
             copy.wait()
-        all_slots = seq_s.shape[0]
-        slot_lane = lax.broadcasted_iota(jnp.int32, (1, all_slots), 1)
         seq_row = seq_v[...].reshape(1, all_slots)
         token = lax.broadcasted_iota(jnp.int32, (1, block_len), 1).astype(jnp.float32)
         for j in range(slots):
@@ -271,6 +266,12 @@
             length = len_s[jnp.maximum(seq, 0)].astype(jnp.float32)
             valid = length - rank * float(block_len)
             live[j : j + 1, :] = jnp.where(token < valid, 1.0, 0.0)
+
+    span = LANES // head_count
+    assert slots <= span
+    first_seq = seq_s[base]
+    lane = lax.broadcasted_iota(jnp.int32, (head_count, LANES), 1)
+    seq_lane = lane - span * lax.broadcasted_iota(jnp.int32, (head_count, LANES), 0)
 
     def own_at(m):
         return m if n_mp == 2 else lax.rem(m + n_mp - mp, n_mp)
@@ -288,13 +289,16 @@
             block = values[:, b * block_len : (b + 1) * block_len] * live[pl.ds(j, 1), :]
             rewards[j] = block
             sums = jnp.sum(block, axis=1, keepdims=True)
-            seq_acc[...] += jnp.where(seq_lane == seq_s[base + j], sums, 0.0)
+            seq = seq_s[base + j]
+            place = jnp.where(seq < 0, LANES, seq - first_seq)
+            seq_acc[...] += jnp.where(seq_lane == place, sums, 0.0)
 
     with jax.named_scope("fin0"):
         for g in range(n_groups - 1):
             finish(g)
     with jax.named_scope("finl"):
         finish(n_groups - 1)
+    sum_row[...] = jnp.sum(seq_acc[...], axis=0, keepdims=True)
     for k in range(n_dp - 1, 0, -1):
         sum_copy(k).start()
 
@@ -305,9 +309,8 @@
     lax.fori_loop(0, n_dp, fill, 0, unroll=n_dp <= 16)
     for k in range(n_dp - 1, 0, -1):
         rew_copy(k).start()
-    recv_sum[dp] = seq_acc[...]
+    recv_sum[dp] = sum_row[...]
     recv_rew[dp] = rewards[send_idx[dp]].astype(recv_rew.dtype)
-    dest_row = dest_v[...].reshape(1, all_slots)
     sources = []
     for q in range(OWN_CAP):
         place = jnp.max(jnp.where(dest_row == dp * OWN_CAP + q, slot_lane, 0))
@@ -316,9 +319,24 @@
 
     with jax.named_scope("sumw"):
         wait_all(recv_sum, sum_recv)
-    totals = recv_sum[0]
-    for s in range(1, n_dp):
-        totals = totals + recv_sum[s]
+    tiles = [jnp.zeros((head_count, LANES), jnp.float32) for _ in range(0, adv_buf.shape[1], LANES)]
+    for s in range(n_dp):
+        first = seq_s[s * slots]
+        turned = pltpu.roll(jnp.broadcast_to(recv_sum[s], (head_count, LANES)), lax.rem(first, LANES), 1)
+        local_at = lax.rem(seq_lane - first + LANES * (len(tiles) + 1), LANES)
+        for i in range(len(tiles)):
+            mine = local_at < span
+            if len(tiles) > 1:
+                at = local_at + (first - i * LANES)
+                mine = mine & (at >= 0) & (at < LANES)
+            tiles[i] = tiles[i] + jnp.where(mine, turned, 0.0)
+    head_row = lax.broadcasted_iota(jnp.int32, (head_count, LANES), 0)
+    for i, tile in enumerate(tiles):
+        straight = tile
+        for k in range(1, head_count):
+            straight = jnp.where(head_row == k, pltpu.roll(tile, LANES - span * k, 1), straight)
+        tiles[i] = straight
+    totals = jnp.concatenate(tiles, axis=1) if len(tiles) > 1 else tiles[0]
     scores = totals[:, :seq_count] / lengths_row
     worst = jnp.min(scores, axis=0, keepdims=True)
     centred = scores - jnp.mean(scores, axis=0, keepdims=True)
@@ -326,14 +344,17 @@
     spread_mean = jnp.mean(spread, axis=1, keepdims=True)
     worst_mean = jnp.mean(worst, axis=1, keepdims=True)
     penalty_scale = spread_mean + stat_epsilon
-    shifted = (worst - spread / penalty_scale) - (worst_mean - spread_mean / penalty_scale)
+    centre = worst_mean - spread_mean / penalty_scale
+    shifted = (worst - spread / penalty_scale) - centre
     variance = jnp.mean(shifted * shifted, axis=1, keepdims=True)
-    adv_buf[...] = jnp.zeros_like(adv_buf)
-    adv_buf[0:1, :seq_count] = shifted * lax.rsqrt(variance + stat_epsilon)
     width = adv_buf.shape[1]
     seq_local = adv_out.shape[1]
-    turned = pltpu.roll(adv_buf[...], width - dp * seq_local, 1)
-    adv_out[...] = turned[0:1, :seq_local]
+    adv_buf[...] = jnp.zeros_like(adv_buf)
+    adv_buf[0:1, :seq_count] = worst
+    adv_buf[1:2, :seq_count] = spread
+    turned = pltpu.roll(adv_buf[...], width - dp * seq_local, 1)[:, :seq_local]
+    own = (turned[0:1] - turned[1:2] / penalty_scale) - centre
+    adv_out[...] = own * lax.rsqrt(variance + stat_epsilon)
     with jax.named_scope("reww"):
         wait_all(recv_rew, rew_recv)
     with jax.named_scope("outs"):
@@ -341,9 +362,8 @@
             rewards_out[q] = recv_rew[sources[q]].astype(jnp.float32)
     with jax.named_scope("sends"):
         for off in range(1, n_mp):
-            for g in range(n_groups):
-                part_copy(off, g).wait_send()
-                attn_copy(off, g).wait_send()
+            pltpu.make_async_copy(part.at[0], part.at[0], part_send.at[off - 1]).wait()
+            pltpu.make_async_copy(attn.at[0], attn.at[0], attn_send.at[off - 1]).wait()
         wait_all(recv_sum, sum_send)
         wait_all(recv_rew, rew_send)
 
@@ -359,7 +379,8 @@
         copy.wait()
 
 
-REW = jnp.bfloat16
+LEAD = 2
+REW = jnp.float32
 
 
 def local(n_dp, n_mp, hidden, attn_out, out_proj, norm_gain, reward_proj, block_seq, block_dest, lengths):
@@ -395,27 +416,27 @@
             pltpu.VMEM((n_mp, n_groups, 2 * heads, rows), f32),
             pltpu.VMEM((slots + (-slots) % 8, block_len), f32),
             pltpu.VMEM((slots, heads, block_len), f32),
-            pltpu.VMEM((heads, seq_pad), f32),
+            pltpu.VMEM((heads, LANES), f32),
+            pltpu.VMEM((1, LANES), f32),
             pltpu.VMEM((n_dp, heads, block_len), REW),
-            pltpu.VMEM((n_dp, heads, seq_pad), f32),
+            pltpu.VMEM((n_dp, 1, LANES), f32),
             pltpu.VMEM((n_dp, heads, block_len), REW),
             pltpu.VMEM((8, seq_pad), f32),
             pltpu.SMEM((n_dp,), jnp.int32),
             pltpu.VMEM(norm_gain.shape, f32),
             pltpu.VMEM((heads, n_local), f32),
             pltpu.SMEM(block_seq.shape, jnp.int32),
-            pltpu.SMEM(block_dest.shape, jnp.int32),
             pltpu.SMEM(lengths.shape, jnp.int32),
             pltpu.VMEM(block_seq.shape, jnp.int32),
             pltpu.VMEM(block_dest.shape, jnp.int32),
             pltpu.VMEM(lengths.shape, jnp.int32),
-            dma((8,)),
+            dma((7,)),
             dma((n_mp, 2)),
             dma((3,)),
             dma,
+            dma((n_mp - 1,)),
             dma((n_mp - 1, n_groups)),
-            dma((n_mp - 1, n_groups)),
-            dma((n_mp - 1, n_groups)),
+            dma((n_mp - 1,)),
             dma((n_mp - 1, n_groups)),
             *[dma] * 4,
         ],

time: 23.7 us -> 23 us (0.970)
  Pallas kernels: 22.9 us -> 22.2 us
    pallas_call x1, Pallas kernels: 22.3 us -> 21.5 us  [local(): pl.pallas_call(functools.partial(kernel, n_dp, n_mp, slots, block_len, se...]
where the time goes in v3:
time: 23 us; the launch traced here: 22.8 us
  Pallas kernels  22.2 us (97%)
  between operations  0.64 us (3%)
    pallas_call x1, Pallas kernels, local(): pl.pallas_call(functools.partial(kernel, n_dp, n_mp, slots, block_len, se...  21.5 us
    pallas_call x1, Pallas kernels, local(): pl.pallas_call(store_kernel, out_shape=(jax.ShapeDtypeStruct(rewards_shap...  0.64 us

profile of v3, /device:TPU:0, one launch (start us, length us, event | category | flops | bytes accessed | tf_op | source)
XLA Modules:
  0.0 22.8 jit_solution(8580724447184401857)
XLA Ops:
  0.6 21.5 %shard_map.95 = (f32[10,8,128]{2,1,0:T(8,128)S(1)}, f32[1,6]{1,0:T(1,128)S(1)}) custom-call(bf16[1920,1024]{1,0:T(8,128)(2,1)} %bitcast.4, bf16[1920,1024]{1,0:T(8,128)(2,1)} %bitcast.5, bf16[2048,1024]{1,0:T(8,128)(2,1)} %w_hbm.1, f32[1024]{0:T(1024)} %gain_hbm.1, f32[8,1024]{1,0:T(8,128)} %bitcast.6, s32[240]{0:T(256)} %seq_hbm.1, s32[240]{0:T(256)} %dest_hbm.1, ...), custom_call_target="tpu_custom_call" | custom-call | tf_op jit(solution)/shard_map/pallas_call | solution.py:404
  22.2 0.6 %shard_map.96 = (f32[10,8,128]{2,1,0:T(8,128)}, f32[1,6]{1,0:T(1,128)}) custom-call(f32[10,8,128]{2,1,0:T(8,128)S(1)} %get-tuple-element.6.rewards_ref, f32[1,6]{1,0:T(1,128)S(1)} %get-tuple-element.7.adv_ref), custom_call_target="tpu_custom_call" | custom-call | tf_op jit(solution)/shard_map/pallas_call | solution.py:456
